TPU v7x, 32 devices: a whole 2x2x4 slice. The times are simulated.
32 devices in a mesh: tm: 32 (over z, y, x, core), prod: 1.
Axes of the slice: x: 2, y: 2, z: 4, core: 2. Of those that a mesh axis runs over, the one named last changes fastest.
Arguments:
- sales_records: float32 [1024, 16, 16, 128], P('tm', 'prod'), may hold values from -6 to 6
- day_month: int32 [1024], replicated, may hold values from 0 to 31, as said below
- month_year: int32 [32], replicated, may hold values from 0 to 3, never falling along the last dimension, each value on 1 to 16 neighbouring positions
- product_category: int32 [16], replicated, may hold values from 0 to 31
- store_region: int32 [16], replicated, may hold values from 0 to 3
Outputs:
- month_detail: float32 [32, 32, 4, 128], P('tm', 'prod')
- month_category: float32 [32, 32, 128], P('tm', 'prod')
- month_region: float32 [32, 4, 128], P('tm')
- month_totals: float32 [32, 128], P('tm')
- year_detail: float32 [4, 32, 4, 128], replicated
- year_category: float32 [4, 32, 128], replicated
- year_region: float32 [4, 4, 128], replicated
- year_totals: float32 [4, 128], replicated
Inputs may be any that keep to these rules, and one draw needn't show every extreme that they name: `day_month`: never falls along the days; month m, for m of 1 to 31, begins at a day from m * 32 - 31 // 2 to m * 32 + 31 // 2, and both ends of that range are taken in every draw. `month_year`: never falls along the months; every year has 1 to 16 months, one exactly that many.
All inputs are finite; a program needn't handle non-finite values.
Results may differ from a plain program's by a relative error of at most 0.0001.
Values sent between devices are 32-bit elements; how exact they have to be, the bound alone decides.
A program may use at most 64 MiB of HBM per device.

v0:
```python
import functools

import jax
import jax.numpy as jnp
from jax import lax
from jax.experimental import pallas as pl
from jax.experimental.pallas import tpu as pltpu
from jax.sharding import PartitionSpec as P

MON_DEV = 1
CATEGORY_COUNT = 32
REGION_COUNT = 4


def with_halo(block, sides, width):
    for axis, dim in sides:
        count = lax.axis_size(axis)
        forward = [(i, i + 1) for i in range(count - 1)]
        backward = [(target, source) for source, target in forward]
        low = lax.ppermute(
            lax.slice_in_dim(block, block.shape[dim] - width, None, axis=dim), axis, forward
        )
        high = lax.ppermute(lax.slice_in_dim(block, 0, width, axis=dim), axis, backward)
        block = jnp.concatenate([low, block, high], axis=dim)
    return block


def onehot(labels, width):
    return (labels[:, None] == jnp.arange(width, dtype=jnp.int32)[None, :]).astype(jnp.float32)


def scaled(sums, counts):
    return sums / jnp.sqrt(counts)


def shards(sales_records, day_month, month_year, product_category, store_region):
    highest = lax.Precision.HIGHEST
    day_dev = sales_records.shape[0]
    prod_dev = sales_records.shape[1]
    stores = float(sales_records.shape[2])
    month_width = month_year.shape[0]
    year_width = max(month_width // 8, 2)
    cats_dev = CATEGORY_COUNT // lax.axis_size("prod")
    products = float(prod_dev * lax.axis_size("prod"))
    time_index = lax.axis_index("tm")
    prod_index = lax.axis_index("prod")
    month_hot = onehot(day_month, month_width)
    year_hot = onehot(month_year, year_width)
    category_hot = onehot(product_category, CATEGORY_COUNT)
    region_hot = onehot(store_region, REGION_COUNT)
    local_products = lax.dynamic_slice_in_dim(category_hot, prod_index * prod_dev, prod_dev, 0)
    by_region = jnp.einsum("dpsq,sr->dprq", sales_records, region_hot, precision=highest)
    by_category = jnp.einsum("dprq,pc->dcrq", by_region, local_products, precision=highest)
    month_days = jnp.sum(month_hot, 0)
    year_days = jnp.dot(month_days, year_hot, precision=highest)
    category_size = jnp.sum(category_hot, 0)
    region_size = jnp.sum(region_hot, 0)
    own_days = lax.dynamic_slice_in_dim(month_days, time_index * MON_DEV, MON_DEV, 0)
    own_sizes = lax.dynamic_slice_in_dim(category_size, prod_index * cats_dev, cats_dev, 0)
    local_labels = lax.dynamic_slice_in_dim(day_month, time_index * day_dev, day_dev, 0)
    window_ids = time_index - 1 + jnp.arange(3, dtype=jnp.int32)
    window_hot = (local_labels[:, None] == window_ids[None, :]).astype(jnp.float32)
    partial_value = jnp.einsum("dcrq,dk->kcrq", by_category, window_hot, precision=highest)
    clipped = jnp.clip(window_ids, 0, month_width - 1)
    inside = ((window_ids >= 0) & (window_ids < month_width)).astype(jnp.float32)
    source_years = onehot(month_year[clipped], year_width) * inside[:, None]
    padded = with_halo(partial_value, (("tm", 0),), 1)
    summed = padded[0:1] + padded[2:3] + padded[4:5]
    detail = lax.psum_scatter(summed, "prod", scatter_dimension=1, tiled=True)
    year_part = jnp.einsum("mcrq,my->ycrq", partial_value, source_years, precision=highest)
    year_cube = lax.psum(year_part, ("tm", "prod"))
    cell = own_days[:, None, None] * own_sizes[None, :, None] * region_size[None, None, :]
    month_detail = scaled(detail, jnp.maximum(cell, 1.0)[..., None])
    month_cat = jnp.sum(detail, 2)
    month_category = scaled(
        month_cat, jnp.maximum(own_days[:, None] * own_sizes[None, :] * stores, 1.0)[..., None]
    )
    month_reg = lax.psum(jnp.sum(detail, 1), "prod")
    month_region = scaled(
        month_reg, jnp.maximum(own_days[:, None] * products * region_size[None, :], 1.0)[..., None]
    )
    month_totals = scaled(jnp.sum(month_reg, 1), (own_days * products * stores)[:, None])
    year_cell = year_days[:, None, None] * category_size[None, :, None] * region_size[None, None, :]
    year_detail = scaled(year_cube, jnp.maximum(year_cell, 1.0)[..., None])
    year_cat = jnp.sum(year_cube, 2)
    year_category = scaled(
        year_cat, jnp.maximum(year_days[:, None] * category_size[None, :] * stores, 1.0)[..., None]
    )
    year_reg = jnp.sum(year_cube, 1)
    year_region = scaled(
        year_reg, jnp.maximum(year_days[:, None] * products * region_size[None, :], 1.0)[..., None]
    )
    year_totals = scaled(jnp.sum(year_reg, 1), (year_days * products * stores)[:, None])
    return (
        month_detail,
        month_category,
        month_region,
        month_totals,
        year_detail,
        year_category,
        year_region,
        year_totals,
    )


MESH = pl.DeviceIdType.MESH
TILE = 8
LANES = 128
CHUNK = 4


def three_parts(value):
    high = value.astype(jnp.bfloat16)
    rest = value - high.astype(jnp.float32)
    middle = rest.astype(jnp.bfloat16)
    low = (rest - middle.astype(jnp.float32)).astype(jnp.bfloat16)
    return high, middle, low


def spread(labels_ref, count, index):
    result = jnp.zeros(index.shape, jnp.int32)
    for i in range(count):
        result = jnp.where(index == i, labels_ref[i], result)
    return result


def hot(mask):
    return jnp.where(mask, 1.0, 0.0)


def bits(count):
    return count.bit_length() - 1


def cube_kernel(
    n, days, products, stores, months, years,
    sales, label_hbm, grid_hbm, year_hbm, category_hbm, region_hbm,
    month_detail, month_category, month_region, month_totals,
    year_detail, year_category, year_region, year_totals,
    day_month, day_grid, month_year, product_category, store_region,
    facts, by_store, window, pieces, arrived, totals, from_low, from_high, maps, factors,
    label_sem, fact_sem,
    piece_send, piece_recv, total_send, total_recv, low_send, low_recv, high_send, high_recv,
):
    me = lax.axis_index("tm")
    chunks = products // CHUNK
    rows = products * REGION_COUNT

    def fetch(c):
        return pltpu.make_async_copy(sales.at[:, pl.ds(c * CHUNK, CHUNK)], facts.at[c], fact_sem.at[c])

    sources = (label_hbm, year_hbm, region_hbm, category_hbm, grid_hbm)
    targets = (day_month, month_year, store_region, product_category, day_grid)
    labels_in = [
        pltpu.make_async_copy(source, target, label_sem.at[i])
        for i, (source, target) in enumerate(zip(sources, targets))
    ]
    for copy in labels_in:
        copy.start()
    for c in range(chunks):
        fetch(c).start()

    barrier = pltpu.get_barrier_semaphore()

    @pl.loop(1, n)
    def _(i):
        pl.semaphore_signal(barrier, 1, device_id={"tm": lax.rem(me + i, n)}, device_id_type=MESH)

    for copy in labels_in:
        copy.wait()
    lane = lax.broadcasted_iota(jnp.int32, (rows, products * stores), 1)
    row = lax.broadcasted_iota(jnp.int32, (rows, products * stores), 0)
    region_of = spread(store_region, stores, lane[:1] & (stores - 1))
    to_region = hot(
        ((row >> bits(REGION_COUNT)) == (lane >> bits(stores))) & ((row & (REGION_COUNT - 1)) == region_of)
    ).astype(jnp.bfloat16)

    for c in range(chunks):
        fetch(c).wait()

        @pl.loop(0, 2)
        def _(half):
            per = CHUNK // 2
            sums = [jnp.zeros((per * stores, LANES), jnp.float32) for _ in range(3)]
            for d in range(days):
                value = facts[c, d, pl.ds(half * per, per)].reshape(per * stores, LANES)
                place = day_month[me * days + d] - me + 1
                for k in range(3):
                    sums[k] = sums[k] + value * jnp.where(place == k, 1.0, 0.0)
            for k in range(3):
                by_store[k, pl.ds(pl.multiple_of((c * 2 + half) * per * stores, per * stores), per * stores)] = sums[k]

    held = []
    for k in range(3):
        part = jnp.zeros((rows, LANES), jnp.float32)
        for piece in three_parts(by_store[k])[::-1]:
            part = part + jnp.dot(to_region, piece, preferred_element_type=jnp.float32)
        held.append(part)
        window[k] = part
    labels = [month_year[jnp.clip(me - 1 + k, 0, months - 1)] for k in range(3)]
    for y in range(years):
        total = jnp.zeros((rows, LANES), jnp.float32)
        for k in range(3):
            total = total + held[k] * jnp.where(labels[k] == y, 1.0, 0.0)
        blocks = rows // TILE
        pieces[y * blocks : (y + 1) * blocks] = total.reshape(blocks, TILE, LANES)

    pl.semaphore_wait(barrier, n - 1)

    @pl.loop(1, n)
    def _(i):
        other = lax.rem(me + i, n)
        pltpu.make_async_remote_copy(
            pieces.at[other], arrived.at[me], piece_send, piece_recv, device_id={"tm": other}, device_id_type=MESH
        ).start()

    below, above = jnp.maximum(me - 1, 0), jnp.minimum(me + 1, n - 1)
    to_below = pltpu.make_async_remote_copy(
        window.at[0], from_high, low_send, low_recv, device_id={"tm": below}, device_id_type=MESH
    )
    to_above = pltpu.make_async_remote_copy(
        window.at[2], from_low, high_send, high_recv, device_id={"tm": above}, device_id_type=MESH
    )

    @pl.when(me > 0)
    def _():
        to_below.start()

    @pl.when(me < n - 1)
    def _():
        to_above.start()

    fill_maps(
        me, products, stores, months, years,
        day_grid, month_year, product_category, store_region, maps, factors,
    )
    arrived[me] = pieces[me]
    everything = pl.ds(0, n - 1)
    pltpu.make_async_copy(arrived.at[everything], arrived.at[everything], piece_recv).wait()
    sums = [arrived[j] for j in range(n)]
    while len(sums) > 1:
        sums = [a + b for a, b in zip(sums[::2], sums[1::2])]
    totals[me] = sums[0]

    @pl.loop(1, n)
    def _(i):
        other = lax.rem(me + i, n)
        pltpu.make_async_remote_copy(
            totals.at[me], totals.at[me], total_send, total_recv, device_id={"tm": other}, device_id_type=MESH
        ).start()

    @pl.when(me > 0)
    def _():
        to_below.wait_send()
        to_above.wait_recv()
        window[1] += from_low[...]

    @pl.when(me < n - 1)
    def _():
        to_above.wait_send()
        to_below.wait_recv()
        window[1] += from_high[...]

    def place(value, period, refs):
        parts = jnp.concatenate(three_parts(value), 0)
        mapped = jnp.dot(maps[...], parts, preferred_element_type=jnp.float32) * factors[period]
        first = 0
        for ref, count in zip(refs, (CATEGORY_COUNT * REGION_COUNT, CATEGORY_COUNT, REGION_COUNT, 1)):
            begin = max(period - 1, 0) * count
            ref[begin : begin + count] = mapped[first : first + count]
            first += count

    place(window[1], 0, (month_detail, month_category, month_region, month_totals))
    pltpu.make_async_copy(pieces.at[everything], pieces.at[everything], piece_send).wait()
    pltpu.make_async_copy(totals.at[everything], totals.at[everything], total_recv).wait()
    for y in range(years):
        value = totals[pl.ds(y * (rows // TILE), rows // TILE)].reshape(rows, LANES)
        place(value, y + 1, (year_detail, year_category, year_region, year_totals))
    pltpu.make_async_copy(totals.at[everything], totals.at[everything], total_send).wait()


def fill_maps(
    me, products, stores, months, years,
    day_grid, month_year, product_category, store_region, maps, factors,
):
    rows = products * REGION_COUNT
    shift, low = bits(REGION_COUNT), REGION_COUNT - 1
    lane = lax.broadcasted_iota(jnp.int32, (1, rows), 1)
    lane_category = spread(product_category, products, lane >> shift)
    lane_region = lane & low

    def row(count):
        return lax.broadcasted_iota(jnp.int32, (count, rows), 0)

    cells = CATEGORY_COUNT * REGION_COUNT
    to_cell = hot(((row(cells) >> shift) == lane_category) & ((row(cells) & low) == lane_region))
    to_cat = hot(row(CATEGORY_COUNT) == lane_category)
    to_reg = hot((row(TILE) == lane_region) | (row(TILE) == REGION_COUNT))
    cell_cat = jnp.sum(to_cell, 1, keepdims=True)
    cat_size = jnp.sum(to_cat, 1, keepdims=True) * (1.0 / REGION_COUNT)
    region_size = []
    for r in range(REGION_COUNT):
        size = jnp.int32(0)
        for s in range(stores):
            size = size + jnp.where(store_region[s] == r, 1, 0)
        region_size.append(size.astype(jnp.float32))

    def sizes(count):
        place = lax.broadcasted_iota(jnp.int32, (count, 1), 0) & low
        result = jnp.zeros((count, 1), jnp.float32)
        for r in range(REGION_COUNT):
            result = jnp.where(place == r, region_size[r], result)
        return result

    cell_reg, reg_size = sizes(cells), sizes(TILE)
    joined = jnp.concatenate([to_cell, to_cat, to_reg], 0)
    maps[...] = jnp.concatenate([joined] * 3, 1).astype(jnp.bfloat16)
    days = day_grid[...]
    years_of = jnp.zeros(days.shape, jnp.int32)
    for m in range(months):
        years_of = jnp.where(days == m, month_year[m], years_of)
    last = lax.broadcasted_iota(jnp.int32, (TILE, 1), 0)
    for i, mask in enumerate([days == me] + [years_of == y for y in range(years)]):
        period = jnp.sum(jnp.sum(hot(mask), 1, keepdims=True), 0, keepdims=True)
        tail = jnp.where(
            last == REGION_COUNT,
            period * float(products * stores),
            jnp.maximum(period * float(products) * reg_size, 1.0),
        )
        counts = jnp.concatenate(
            [
                jnp.maximum(period * cell_cat * cell_reg, 1.0),
                jnp.maximum(period * cat_size * float(stores), 1.0),
                tail,
            ],
            0,
        )
        factors[i] = jnp.broadcast_to(1.0 / jnp.sqrt(counts), (counts.shape[0], LANES))


def finish_kernel(*refs):
    count = len(refs) // 2
    copies = [pltpu.make_async_copy(refs[i], refs[count + i], refs[-1].at[i]) for i in range(count)]
    for copy in copies:
        copy.start()
    for copy in copies:
        copy.wait()


def kernels(sales_records, day_month, month_year, product_category, store_region):
    n = lax.axis_size("tm")
    days, products, stores, _ = sales_records.shape
    months = month_year.shape[0]
    years = max(months // 8, 2)
    rows = products * REGION_COUNT
    f32 = jnp.float32
    hbm = pl.BlockSpec(memory_space=pl.ANY)
    vmem = pl.BlockSpec(memory_space=pltpu.VMEM)
    dma = pltpu.SemaphoreType.DMA
    i32 = jnp.int32
    cells = CATEGORY_COUNT * REGION_COUNT
    lines = cells + CATEGORY_COUNT + TILE
    shapes = [(cells, LANES), (CATEGORY_COUNT, LANES), (REGION_COUNT, LANES), (1, LANES)]
    shapes += [(years * count, LANES) for count, _ in shapes]
    grid = day_month.reshape(-1, LANES)
    results = pl.pallas_call(
        functools.partial(cube_kernel, n, days, products, stores, months, years),
        out_shape=tuple(pltpu.VMEM(s, f32) for s in shapes),
        in_specs=[hbm] * 6,
        out_specs=(vmem,) * 8,
        scratch_shapes=[
            pltpu.SMEM(day_month.shape, i32),
            pltpu.VMEM(grid.shape, i32),
            pltpu.SMEM(month_year.shape, i32),
            pltpu.SMEM(product_category.shape, i32),
            pltpu.SMEM(store_region.shape, i32),
            pltpu.VMEM((products // CHUNK, days, CHUNK, stores, LANES), f32),
            pltpu.VMEM((3, products * stores, LANES), f32),
            pltpu.VMEM((3, rows, LANES), f32),
            pltpu.VMEM((n, TILE, LANES), f32),
            pltpu.VMEM((n, TILE, LANES), f32),
            pltpu.VMEM((n, TILE, LANES), f32),
            pltpu.VMEM((rows, LANES), f32),
            pltpu.VMEM((rows, LANES), f32),
            pltpu.VMEM((lines, 3 * rows), jnp.bfloat16),
            pltpu.VMEM((years + 1, lines, LANES), f32),
            dma((5,)),
            dma((products // CHUNK,)),
        ]
        + [dma] * 8,
        compiler_params=pltpu.CompilerParams(collective_id=0, has_side_effects=True),
        name="cube",
    )(sales_records, day_month, grid, month_year, product_category, store_region)
    outs = pl.pallas_call(
        finish_kernel,
        out_shape=tuple(jax.ShapeDtypeStruct(s, f32) for s in shapes),
        in_specs=[vmem] * 8,
        out_specs=(hbm,) * 8,
        scratch_shapes=[dma((8,))],
        compiler_params=pltpu.CompilerParams(vmem_limit_bytes=2**20),
        name="finish",
    )(*results)
    tails = [(CATEGORY_COUNT, REGION_COUNT, LANES), (CATEGORY_COUNT, LANES), (REGION_COUNT, LANES), (LANES,)]
    return tuple(
        out.reshape((1 if i < 4 else years,) + tails[i % 4]) for i, out in enumerate(outs)
    )


def power(count):
    return count & (count - 1) == 0


def body(*args):
    days, products, stores, lanes = args[0].shape
    n = lax.axis_size("tm")
    tiles = max(args[2].shape[0] // 8, 2) * products * REGION_COUNT // TILE
    fits = (
        lax.axis_size("prod") == 1
        and tiles == n
        and power(n)
        and power(stores)
        and stores % TILE == 0
        and products % CHUNK == 0
        and lanes == LANES
        and args[1].shape[0] % (TILE * LANES) == 0
    )
    return kernels(*args) if fits else shards(*args)


def solution(mesh):
    placed = (P("tm", "prod", None, None), P(), P(), P(), P())
    return jax.shard_map(
        body,
        mesh=mesh,
        in_specs=placed,
        out_specs=(
            P("tm", "prod", None, None),
            P("tm", "prod", None),
            P("tm", None, None),
            P("tm", None),
            P(),
            P(),
            P(),
            P(),
        ),
        check_vma=False,
    )
```

profile of v0, /device:TPU:0, one launch (start us, length us, event | category | flops | bytes accessed | tf_op | source)
XLA Modules:
  0.0 19.3 jit_solution(9860230112679198907)
XLA Ops:
  0.6 17.8 %cube.1 = (f32[128,128]{1,0:T(8,128)S(1)}, f32[32,128]{1,0:T(8,128)S(1)}, f32[4,128]{1,0:T(4,128)S(1)}, f32[1,128]{1,0:T(1,128)S(1)}, f32[512,128]{1,0:T(8,128)S...) custom-call(f32[32,16,16,128]{3,2,1,0:T(8,128)} %sales.1, s32[1024]{0:T(1024)} %label_hbm.1, ...), custom_call_target="tpu_custom_call" | custom-call | tf_op jit(solution)/shard_map/cube/pallas_call | solution.py:366
  18.4 0.8 %finish.1 = (f32[128,128]{1,0:T(8,128)}, f32[32,128]{1,0:T(8,128)}, f32[4,128]{1,0:T(4,128)}, f32[1,128]{1,0:T(1,128)}, f32[512,128]{1,0:T(8,128)}, /*index=5*/f...) custom-call(f32[128,128]{1,0:T(8,128)S(1)} %get-tuple-element.24.refs_0_, f32[32,128]{1,0:T(8,128)S(1)} %get-tuple-element.25.refs_1_, ...), custom_call_target="tpu_custom_call" | custom-call | tf_op jit(solution)/shard_map/finish/pallas_call | solution.py:394
where the time goes:
time: 19.5 us; the launch traced here: 19.3 us
  Pallas kernels  18.6 us (95%)
  between operations  0.64 us (3%)
    pallas_call x1, Pallas kernels, kernels(): pl.pallas_call(functools.partial(cube_kernel, n, days, products, stores,...  17.8 us
    pallas_call x1, Pallas kernels, kernels(): pl.pallas_call(finish_kernel, out_shape=tuple((jax.ShapeDtypeStruct(s, f3...  0.83 us

commit v1 on v0

--- a/solution.py
+++ b/solution.py
@@ -132,25 +132,57 @@
     return count.bit_length() - 1
 
 
+def source_ranges(n, months, years):
+    longest = 2 * months // years
+    result = []
+    for y in range(years):
+        first = max(y, months - longest * (years - y))
+        last = min(longest * (y + 1), months - (years - 1 - y)) - 1
+        result.append((max(first - 1, 0), min(last + 1, n - 1)))
+    return result
+
+
 def cube_kernel(
     n, days, products, stores, months, years,
-    sales, label_hbm, grid_hbm, year_hbm, category_hbm, region_hbm,
+    sales, grid_hbm, year_hbm, category_hbm, region_hbm,
     month_detail, month_category, month_region, month_totals,
     year_detail, year_category, year_region, year_totals,
-    day_month, day_grid, month_year, product_category, store_region,
-    facts, by_store, window, pieces, arrived, totals, from_low, from_high, maps, factors,
+    day_row, day_grid, month_year, product_category, store_region,
+    facts, window, pieces, arrived, totals, from_low, from_high, maps, factors,
     label_sem, fact_sem,
     piece_send, piece_recv, total_send, total_recv, low_send, low_recv, high_send, high_recv,
 ):
     me = lax.axis_index("tm")
     chunks = products // CHUNK
     rows = products * REGION_COUNT
+    group = CHUNK * REGION_COUNT // TILE
+    per = years * group
+    spacing = n // 2 // per
+    owners = [n // 4 + t * spacing + spacing - 1 for t in range(per)]
+    ranges = source_ranges(n, months, years)
+    within = [(me >= low) & (me <= high) for low, high in ranges]
+
+    def owns(device):
+        place = device - n // 4
+        return (place >= 0) & (place < n // 2) & (lax.rem(place + n, spacing) == spacing - 1)
+
+    def number(flag):
+        return jnp.where(flag, 1, 0)
+
+    owner = owns(me)
+    far = (me >= n // 2) & jnp.logical_not(owner)
+    mine = jnp.clip((me - n // 4) // spacing, 0, per - 1)
 
     def fetch(c):
         return pltpu.make_async_copy(sales.at[:, pl.ds(c * CHUNK, CHUNK)], facts.at[c], fact_sem.at[c])
 
-    sources = (label_hbm, year_hbm, region_hbm, category_hbm, grid_hbm)
-    targets = (day_month, month_year, store_region, product_category, day_grid)
+    def remote(source, target, send, recv, device):
+        return pltpu.make_async_remote_copy(
+            source, target, send, recv, device_id={"tm": device}, device_id_type=MESH
+        )
+
+    sources = (grid_hbm.at[me * days // LANES], year_hbm, region_hbm, category_hbm, grid_hbm)
+    targets = (day_row, month_year, store_region, product_category, day_grid)
     labels_in = [
         pltpu.make_async_copy(source, target, label_sem.at[i])
         for i, (source, target) in enumerate(zip(sources, targets))
@@ -162,65 +194,110 @@
 
     barrier = pltpu.get_barrier_semaphore()
 
-    @pl.loop(1, n)
-    def _(i):
-        pl.semaphore_signal(barrier, 1, device_id={"tm": lax.rem(me + i, n)}, device_id_type=MESH)
+    def greet(device):
+        pl.semaphore_signal(barrier, 1, device_id={"tm": device}, device_id_type=MESH)
+
+    @pl.when(owner)
+    def _():
+        @pl.loop(0, n)
+        def _(i):
+            @pl.when(i != me)
+            def _():
+                greet(i)
+
+        @pl.loop(0, n)
+        def _(i):
+            unused = False
+            for y, (low, high) in enumerate(ranges):
+                unused = unused | ((mine // group == y) & ((i < low) | (i > high)))
+
+            @pl.when(unused)
+            def _():
+                for c in range(chunks):
+                    arrived[c, i] = jnp.zeros((TILE, LANES), jnp.float32)
+
+    @pl.when(jnp.logical_not(owner))
+    def _():
+        for device in owners:
+            greet(device)
+
+        @pl.when((me > 0) & jnp.logical_not(owns(me - 1)))
+        def _():
+            greet(me - 1)
+
+        @pl.when((me < n - 1) & jnp.logical_not(owns(me + 1)))
+        def _():
+            greet(me + 1)
+
+    def meet():
+        @pl.when(owner)
+        def _():
+            pl.semaphore_wait(barrier, n - 1)
+
+        @pl.when(jnp.logical_not(owner))
+        def _():
+            beside = number((me > 0) & jnp.logical_not(owns(me - 1)))
+            beside = beside + number((me < n - 1) & jnp.logical_not(owns(me + 1)))
+            pl.semaphore_wait(barrier, per + beside)
+
+    def send(c):
+        for t, device in enumerate(owners):
+
+            @pl.when(within[t // group] & (me != device))
+            def _():
+                remote(pieces.at[c * per + t], arrived.at[c, me], piece_send, piece_recv.at[c], device).start()
 
     for copy in labels_in:
         copy.wait()
-    lane = lax.broadcasted_iota(jnp.int32, (rows, products * stores), 1)
-    row = lax.broadcasted_iota(jnp.int32, (rows, products * stores), 0)
+    across = CHUNK * stores
+    lines = CHUNK * REGION_COUNT
+    lane = lax.broadcasted_iota(jnp.int32, (lines, across), 1)
+    row = lax.broadcasted_iota(jnp.int32, (lines, across), 0)
     region_of = spread(store_region, stores, lane[:1] & (stores - 1))
     to_region = hot(
         ((row >> bits(REGION_COUNT)) == (lane >> bits(stores))) & ((row & (REGION_COUNT - 1)) == region_of)
-    ).astype(jnp.bfloat16)
+    )
+    to_region = jnp.concatenate([to_region] * 3, 1).astype(jnp.bfloat16)
+    labels = [month_year[jnp.clip(me - 1 + k, 0, months - 1)] for k in range(3)]
+    start = lax.rem(me * days, LANES)
 
     for c in range(chunks):
         fetch(c).wait()
-
-        @pl.loop(0, 2)
-        def _(half):
-            per = CHUNK // 2
-            sums = [jnp.zeros((per * stores, LANES), jnp.float32) for _ in range(3)]
-            for d in range(days):
-                value = facts[c, d, pl.ds(half * per, per)].reshape(per * stores, LANES)
-                place = day_month[me * days + d] - me + 1
-                for k in range(3):
-                    sums[k] = sums[k] + value * jnp.where(place == k, 1.0, 0.0)
+        sums = [jnp.zeros((across, LANES), jnp.float32) for _ in range(3)]
+        for d in range(days):
+            value = facts[c, d].reshape(across, LANES)
+            place = day_row[start + d] - me + 1
+            for k in (0, 1) if d < days // 2 else (1, 2):
+                sums[k] = sums[k] + value * jnp.where(place == k, 1.0, 0.0)
+        held = []
+        for k in range(3):
+            parts = jnp.concatenate(three_parts(sums[k]), 0)
+            held.append(jnp.dot(to_region, parts, preferred_element_type=jnp.float32))
+            window[k, c * lines : (c + 1) * lines] = held[k]
+        for y in range(years):
+            total = jnp.zeros((lines, LANES), jnp.float32)
             for k in range(3):
-                by_store[k, pl.ds(pl.multiple_of((c * 2 + half) * per * stores, per * stores), per * stores)] = sums[k]
-
-    held = []
-    for k in range(3):
-        part = jnp.zeros((rows, LANES), jnp.float32)
-        for piece in three_parts(by_store[k])[::-1]:
-            part = part + jnp.dot(to_region, piece, preferred_element_type=jnp.float32)
-        held.append(part)
-        window[k] = part
-    labels = [month_year[jnp.clip(me - 1 + k, 0, months - 1)] for k in range(3)]
-    for y in range(years):
-        total = jnp.zeros((rows, LANES), jnp.float32)
-        for k in range(3):
-            total = total + held[k] * jnp.where(labels[k] == y, 1.0, 0.0)
-        blocks = rows // TILE
-        pieces[y * blocks : (y + 1) * blocks] = total.reshape(blocks, TILE, LANES)
-
-    pl.semaphore_wait(barrier, n - 1)
-
-    @pl.loop(1, n)
-    def _(i):
-        other = lax.rem(me + i, n)
-        pltpu.make_async_remote_copy(
-            pieces.at[other], arrived.at[me], piece_send, piece_recv, device_id={"tm": other}, device_id_type=MESH
-        ).start()
+                total = total + held[k] * jnp.where(labels[k] == y, 1.0, 0.0)
+            first = c * per + y * group
+            pieces[first : first + group] = total.reshape(group, TILE, LANES)
+
+        @pl.when(far)
+        def _():
+            if c == 0:
+                meet()
+            send(c)
+
+    @pl.when(jnp.logical_not(far))
+    def _():
+        meet()
+
+        @pl.loop(0, chunks)
+        def _(c):
+            send(c)
 
     below, above = jnp.maximum(me - 1, 0), jnp.minimum(me + 1, n - 1)
-    to_below = pltpu.make_async_remote_copy(
-        window.at[0], from_high, low_send, low_recv, device_id={"tm": below}, device_id_type=MESH
-    )
-    to_above = pltpu.make_async_remote_copy(
-        window.at[2], from_low, high_send, high_recv, device_id={"tm": above}, device_id_type=MESH
-    )
+    to_below = remote(window.at[0], from_high, low_send, low_recv, below)
+    to_above = remote(window.at[2], from_low, high_send, high_recv, above)
 
     @pl.when(me > 0)
     def _():
@@ -234,20 +311,46 @@
         me, products, stores, months, years,
         day_grid, month_year, product_category, store_region, maps, factors,
     )
-    arrived[me] = pieces[me]
-    everything = pl.ds(0, n - 1)
-    pltpu.make_async_copy(arrived.at[everything], arrived.at[everything], piece_recv).wait()
-    sums = [arrived[j] for j in range(n)]
-    while len(sums) > 1:
-        sums = [a + b for a, b in zip(sums[::2], sums[1::2])]
-    totals[me] = sums[0]
-
-    @pl.loop(1, n)
-    def _(i):
-        other = lax.rem(me + i, n)
-        pltpu.make_async_remote_copy(
-            totals.at[me], totals.at[me], total_send, total_recv, device_id={"tm": other}, device_id_type=MESH
-        ).start()
+
+    def gather(c):
+        sent = [high - low + 1 - (low <= owners[t] <= high) for t, (low, high) in
+                enumerate(r for r in ranges for _ in range(group))]
+        for count in sorted(set(sent)):
+            is_count = False
+            for t in range(per):
+                if sent[t] == count:
+                    is_count = is_count | (mine == t)
+
+            @pl.when(is_count)
+            def _():
+                everything = arrived.at[c, pl.ds(0, count)]
+                pltpu.make_async_copy(everything, everything, piece_recv.at[c]).wait()
+
+        inside = False
+        for t in range(per):
+            if ranges[t // group][0] <= owners[t] <= ranges[t // group][1]:
+                inside = inside | (mine == t)
+
+        @pl.when(inside)
+        def _():
+            arrived[c, me] = pieces[c * per + mine]
+
+        sums = [arrived[c, j] for j in range(n)]
+        while len(sums) > 1:
+            sums = [a + b for a, b in zip(sums[::2], sums[1::2])]
+        slot = (mine // group) * (rows // TILE) + c * group + lax.rem(mine, group)
+        totals[slot] = sums[0]
+
+        @pl.loop(0, n)
+        def _(i):
+            @pl.when(i != me)
+            def _():
+                remote(totals.at[slot], totals.at[slot], total_send, total_recv, i).start()
+
+    @pl.when(owner)
+    def _():
+        for c in range(chunks - 1):
+            gather(c)
 
     @pl.when(me > 0)
     def _():
@@ -271,12 +374,39 @@
             first += count
 
     place(window[1], 0, (month_detail, month_category, month_region, month_totals))
-    pltpu.make_async_copy(pieces.at[everything], pieces.at[everything], piece_send).wait()
-    pltpu.make_async_copy(totals.at[everything], totals.at[everything], total_recv).wait()
+
+    @pl.when(owner)
+    def _():
+        gather(chunks - 1)
+
+    sends = sum(number(flag) for flag in within) * group
+    sends = sends - sum(number(within[t // group] & (me == device)) for t, device in enumerate(owners))
+    for count in range(per + 1):
+
+        @pl.when(sends == count)
+        def _():
+            if count:
+                sent = pieces.at[pl.ds(0, count * chunks)]
+                pltpu.make_async_copy(sent, sent, piece_send).wait()
+
+    @pl.when(owner)
+    def _():
+        others = totals.at[pl.ds(0, (per - 1) * chunks)]
+        pltpu.make_async_copy(others, others, total_recv).wait()
+
+    @pl.when(jnp.logical_not(owner))
+    def _():
+        pltpu.make_async_copy(totals, totals, total_recv).wait()
+
     for y in range(years):
         value = totals[pl.ds(y * (rows // TILE), rows // TILE)].reshape(rows, LANES)
         place(value, y + 1, (year_detail, year_category, year_region, year_totals))
-    pltpu.make_async_copy(totals.at[everything], totals.at[everything], total_send).wait()
+
+    @pl.when(owner)
+    def _():
+        for c in range(chunks):
+            others = pieces.at[pl.ds(0, n - 1)]
+            pltpu.make_async_copy(others, others, total_send).wait()
 
 
 def fill_maps(
@@ -366,19 +496,18 @@
     results = pl.pallas_call(
         functools.partial(cube_kernel, n, days, products, stores, months, years),
         out_shape=tuple(pltpu.VMEM(s, f32) for s in shapes),
-        in_specs=[hbm] * 6,
+        in_specs=[hbm] * 5,
         out_specs=(vmem,) * 8,
         scratch_shapes=[
-            pltpu.SMEM(day_month.shape, i32),
+            pltpu.SMEM((LANES,), i32),
             pltpu.VMEM(grid.shape, i32),
             pltpu.SMEM(month_year.shape, i32),
             pltpu.SMEM(product_category.shape, i32),
             pltpu.SMEM(store_region.shape, i32),
             pltpu.VMEM((products // CHUNK, days, CHUNK, stores, LANES), f32),
-            pltpu.VMEM((3, products * stores, LANES), f32),
             pltpu.VMEM((3, rows, LANES), f32),
             pltpu.VMEM((n, TILE, LANES), f32),
-            pltpu.VMEM((n, TILE, LANES), f32),
+            pltpu.VMEM((products // CHUNK, n, TILE, LANES), f32),
             pltpu.VMEM((n, TILE, LANES), f32),
             pltpu.VMEM((rows, LANES), f32),
             pltpu.VMEM((rows, LANES), f32),
@@ -387,10 +516,11 @@
             dma((5,)),
             dma((products // CHUNK,)),
         ]
-        + [dma] * 8,
+        + [dma, dma((products // CHUNK,))]
+        + [dma] * 6,
         compiler_params=pltpu.CompilerParams(collective_id=0, has_side_effects=True),
         name="cube",
-    )(sales_records, day_month, grid, month_year, product_category, store_region)
+    )(sales_records, grid, month_year, product_category, store_region)
     outs = pl.pallas_call(
         finish_kernel,
         out_shape=tuple(jax.ShapeDtypeStruct(s, f32) for s in shapes),
@@ -417,12 +547,15 @@
     fits = (
         lax.axis_size("prod") == 1
         and tiles == n
+        and args[2].shape[0] == n
         and power(n)
         and power(stores)
         and stores % TILE == 0
         and products % CHUNK == 0
         and lanes == LANES
         and args[1].shape[0] % (TILE * LANES) == 0
+        and LANES % days == 0
+        and n // 2 % (tiles * CHUNK // products) == 0
     )
     return kernels(*args) if fits else shards(*args)
 

time: 19.5 us -> 17.6 us (0.903)
  Pallas kernels: 18.6 us -> 16.8 us
    pallas_call x1, Pallas kernels: 17.8 us -> 16 us  [kernels(): pl.pallas_call(functools.partial(cube_kernel, n, days, products, stores,...]
where the time goes in v1:
time: 17.6 us; the launch traced here: 17.5 us
  Pallas kernels  16.8 us (95%)
  between operations  0.64 us (4%)
    pallas_call x1, Pallas kernels, kernels(): pl.pallas_call(functools.partial(cube_kernel, n, days, products, stores,...  16 us
    pallas_call x1, Pallas kernels, kernels(): pl.pallas_call(finish_kernel, out_shape=tuple((jax.ShapeDtypeStruct(s, f3...  0.83 us

profile of v1, /device:TPU:0, one launch (start us, length us, event | category | flops | bytes accessed | tf_op | source)
XLA Modules:
  0.0 17.5 jit_solution(3898409480046039667)
XLA Ops:
  0.6 16.0 %cube.1 = (f32[128,128]{1,0:T(8,128)S(1)}, f32[32,128]{1,0:T(8,128)S(1)}, f32[4,128]{1,0:T(4,128)S(1)}, f32[1,128]{1,0:T(1,128)S(1)}, f32[512,128]{1,0:T(8,128)S...) custom-call(f32[32,16,16,128]{3,2,1,0:T(8,128)} %sales.1, s32[8,128]{1,0:T(8,128)} %bitcast.7, ...), custom_call_target="tpu_custom_call" | custom-call | tf_op jit(solution)/shard_map/cube/pallas_call | solution.py:496
  16.6 0.8 %finish.1 = (f32[128,128]{1,0:T(8,128)}, f32[32,128]{1,0:T(8,128)}, f32[4,128]{1,0:T(4,128)}, f32[1,128]{1,0:T(1,128)}, f32[512,128]{1,0:T(8,128)}, /*index=5*/f...) custom-call(f32[128,128]{1,0:T(8,128)S(1)} %get-tuple-element.24.refs_0_, f32[32,128]{1,0:T(8,128)S(1)} %get-tuple-element.25.refs_1_, ...), custom_call_target="tpu_custom_call" | custom-call | tf_op jit(solution)/shard_map/finish/pallas_call | solution.py:524
